TPU v7x, 32 devices: a whole 2x2x4 slice. The times are simulated.
32 devices in a mesh: row: 4 (over y, core), col: 8 (over z, x).
Axes of the slice: x: 2, y: 2, z: 4, core: 2. Of those that a mesh axis runs over, the one named last changes fastest.
Arguments:
- matrix: float32 [4096, 4096], P('row', 'col'), may hold values from -12 to 12, as said below
Outputs:
- sign_estimate: float32 [4096, 4096], P('row', 'col')
Inputs may be any that keep to these rules, and one draw needn't show every extreme that they name: `matrix`: symmetric; the magnitudes of its eigenvalues, divided by the root mean square of all its eigenvalues, lie between 0.4 and 1.7.
All inputs are finite; a program needn't handle non-finite values.
Results may differ from a plain program's by a relative error of at most 0.0002.
Values sent between devices are 32-bit elements; how exact they have to be, the bound alone decides.
A program may use at most 64 MiB of HBM per device.

v0:
```python
import functools

import jax
import jax.numpy as jnp
from jax import lax
from jax.experimental import pallas as pl
from jax.experimental.pallas import tpu as pltpu
from jax.sharding import PartitionSpec as P

ITERS = 2
PIECES = 8
MESH = pl.DeviceIdType.MESH


class Gather:
    def __init__(self, axis, size, src, slot, line, pair, sends, copy_sem, swapped=0):
        self.axis, self.src, self.slot = axis, src, slot
        self.line, self.pair, self.sends, self.copy_sem = line, pair, sends, copy_sem
        me = lax.axis_index(axis)
        self.spots = size // 2
        self.spot, self.side = me // 2, lax.rem(me, 2)
        self.partner = me + 1 - 2 * self.side
        self.left, self.right = me - 2, me + 2
        self.pieces = line.shape[1]
        self.depth = src.shape[0] // self.pieces
        self.swapped = swapped

    def ends(self):
        return ((self.left, self.spot > 0), (self.right, self.spot < self.spots - 1))

    def greet(self, barrier):
        pl.semaphore_signal(barrier, inc=1, device_id={self.axis: self.partner}, device_id_type=MESH)
        for target, there in self.ends():
            @pl.when(there)
            def _():
                pl.semaphore_signal(barrier, inc=1, device_id={self.axis: target}, device_id_type=MESH)

    def peers(self):
        return 1 + sum(there.astype(jnp.int32) for _, there in self.ends())

    def part(self, ref, piece):
        return ref.at[pl.ds(piece * self.depth, self.depth), :]

    def copy(self, spot, piece, way, own, other=False):
        side = 1 - self.side if other else self.side
        dst = self.part(self.slot(2 * spot + side), piece)
        src = self.part(self.src, piece) if own else dst
        sems = self.pair if way == 2 or other else self.line
        target = (self.left, self.right, self.partner)[way]
        return pltpu.make_async_remote_copy(
            src_ref=src, dst_ref=dst, send_sem=self.sends.at[way + 3 * other, spot, piece],
            recv_sem=sems.at[spot, piece], device_id={self.axis: target}, device_id_type=MESH)

    def arrive(self, spot, piece, side, sems):
        dst = self.part(self.slot(2 * spot + side), piece)
        pltpu.make_async_remote_copy(
            src_ref=dst, dst_ref=dst, send_sem=self.sends.at[2, spot, piece], recv_sem=sems.at[spot, piece],
            device_id={self.axis: self.partner}, device_id_type=MESH).wait_recv()

    def onward(self, act, spot, piece, ways, own, other=False):
        for way in ways:
            @pl.when(self.ends()[way][1])
            def _():
                getattr(self.copy(spot, piece, way, own, other), act)()

    def far_spots(self, far):
        return ((0, self.spot + far, self.spot + far < self.spots), (1, self.spot - far, self.spot >= far))

    def begin(self):
        self.keep = pltpu.make_async_copy(self.src, self.slot(2 * self.spot + self.side), self.copy_sem)
        self.keep.start()
        for piece in range(self.pieces):
            self.copy(self.spot, piece, 2, True).start()
            self.onward("start", self.spot, piece, (0, 1), True)

    def cross(self):
        for piece in range(self.swapped):
            self.arrive(self.spot, piece, 1 - self.side, self.pair)
            self.onward("start", self.spot, piece, (0, 1), False, True)

    def relay(self, far, piece):
        for way, spot, here in self.far_spots(far):
            @pl.when(here)
            def _():
                self.arrive(spot, piece, self.side, self.line)
                self.onward("start", spot, piece, (way,), False)
                if piece >= self.swapped:
                    self.copy(spot, piece, 2, False).start()

    def relay_crossed(self, far):
        for piece in range(self.swapped):
            for way, spot, here in self.far_spots(far):
                @pl.when(here)
                def _():
                    self.arrive(spot, piece, 1 - self.side, self.pair)
                    self.onward("start", spot, piece, (way,), False, True)

    def finish(self):
        self.keep.wait()
        for piece in range(self.pieces):
            crossed = piece < self.swapped
            if not crossed:
                self.arrive(self.spot, piece, 1 - self.side, self.pair)
            self.copy(self.spot, piece, 2, True).wait_send()
            self.onward("wait_send", self.spot, piece, (0, 1), True)
            if crossed:
                self.onward("wait_send", self.spot, piece, (0, 1), False, True)
        for far in range(1, self.spots):
            for piece in range(self.pieces):
                crossed = piece < self.swapped
                for way, spot, here in self.far_spots(far):
                    @pl.when(here)
                    def _():
                        if not crossed:
                            self.arrive(spot, piece, 1 - self.side, self.pair)
                            self.copy(spot, piece, 2, False).wait_send()
                        self.onward("wait_send", spot, piece, (way,), False)
                        if crossed:
                            self.onward("wait_send", spot, piece, (way,), False, True)


def run_gathers(gathers):
    barrier = pltpu.get_barrier_semaphore()
    for g in gathers:
        g.greet(barrier)
    pl.semaphore_wait(barrier, sum(g.peers() for g in gathers))
    for g in gathers:
        g.begin()
    for g in gathers:
        g.cross()
    for far in range(1, max(g.spots for g in gathers)):
        for piece in range(PIECES):
            for g in gathers:
                if far < g.spots and piece < g.pieces:
                    g.relay(far, piece)
        for g in gathers:
            if far < g.spots:
                g.relay_crossed(far)
    for g in gathers:
        g.finish()


def down(ref, depth):
    return lambda i: ref.at[pl.ds(pl.multiple_of(i * depth, depth), depth), :]


def across(ref, width):
    return lambda i: ref.at[:, pl.ds(pl.multiple_of(i * width, width), width)]


def both_kernel(row_n, col_n, x_ref, s_ref, rows_ref, cols_ref, stats_ref, *sems):
    depth, width = x_ref.shape
    copies = sems[9]
    run_gathers((
        Gather("col", col_n, s_ref, down(stats_ref, 8), *sems[6:9], copies.at[2]),
        Gather("row", row_n, x_ref, down(cols_ref, depth), *sems[3:6], copies.at[1]),
        Gather("col", col_n, x_ref, across(rows_ref, width), *sems[0:3], copies.at[0], swapped=1),
    ))


def cols_kernel(row_n, x_ref, s_ref, cols_ref, stats_ref, *sems):
    depth = x_ref.shape[0]
    copies = sems[6]
    run_gathers((
        Gather("row", row_n, s_ref, down(stats_ref, 8), *sems[3:6], copies.at[1]),
        Gather("row", row_n, x_ref, down(cols_ref, depth), *sems[0:3], copies.at[0]),
    ))


def sems(size, pieces):
    dma = pltpu.SemaphoreType.DMA
    return [dma((size // 2, pieces)), dma((size // 2, pieces)), dma((5, size // 2, pieces))]


ANY = pl.BlockSpec(memory_space=pl.ANY)


def gather_both(x, stat, row_n, col_n):
    depth, width = x.shape
    return pl.pallas_call(
        functools.partial(both_kernel, row_n, col_n),
        out_shape=(jax.ShapeDtypeStruct((depth, width * col_n), x.dtype),
                   jax.ShapeDtypeStruct((depth * row_n, width), x.dtype),
                   jax.ShapeDtypeStruct((8 * col_n, 128), x.dtype)),
        in_specs=[ANY, ANY], out_specs=(ANY, ANY, ANY),
        scratch_shapes=sems(col_n, PIECES) + sems(row_n, PIECES) + sems(col_n, 1) + [pltpu.SemaphoreType.DMA((3,))],
        compiler_params=pltpu.CompilerParams(collective_id=0, has_side_effects=True),
        name="gather_both",
    )(x, stat)


def gather_cols(x, stat, row_n):
    depth, width = x.shape
    return pl.pallas_call(
        functools.partial(cols_kernel, row_n),
        out_shape=(jax.ShapeDtypeStruct((depth * row_n, width), x.dtype),
                   jax.ShapeDtypeStruct((8 * row_n, 128), x.dtype)),
        in_specs=[ANY, ANY], out_specs=(ANY, ANY),
        scratch_shapes=sems(row_n, PIECES) + sems(row_n, 1) + [pltpu.SemaphoreType.DMA((2,))],
        compiler_params=pltpu.CompilerParams(collective_id=1, has_side_effects=True),
        name="gather_cols",
    )(x, stat)


def dot(a, b):
    return jnp.dot(a, b, preferred_element_type=jnp.float32, precision=lax.Precision.HIGH)


def fold(x):
    return jnp.sum(x.reshape(x.shape[0] // 8, 8, x.shape[1] // 128, 128), axis=(0, 2))


def shards(row_n, col_n, matrix):
    x_iter = matrix
    stat = fold(matrix * matrix)
    for step in range(ITERS):
        rows_panel, cols_panel, stats = gather_both(x_iter, stat, row_n, col_n)
        square = dot(rows_panel, cols_panel)
        square_panel, stats = gather_cols(square, fold(stats), row_n)
        cube = dot(rows_panel, square_panel)
        if step == 0:
            factor = jnp.sqrt(matrix.shape[0] * row_n / jnp.sum(stats))
            x_iter = factor * (1.5 * x_iter - (0.5 * factor * factor) * cube)
        else:
            x_iter = 1.5 * x_iter - 0.5 * cube
    return x_iter


def solution(mesh):
    body = functools.partial(shards, mesh.shape["row"], mesh.shape["col"])
    return jax.shard_map(body, mesh=mesh, in_specs=(P("row", "col"),), out_specs=P("row", "col"), check_vma=False)
```

profile of v0, /device:TPU:0, one launch (start us, length us, event | category | flops | bytes accessed | tf_op | source)
XLA Modules:
  0.0 561.1 jit_solution(16663154306033762317)
XLA Ops:
  0.0 2.7 bitcast_reduce_fusion.s_ref
  2.7 171.9 %gather_both.2 = (f32[1024,4096]{1,0:T(8,128)}, f32[4096,512]{1,0:T(8,128)}, f32[64,128]{1,0:T(8,128)}) custom-call(f32[1024,512]{1,0:T(8,128)} %x_ref.1, f32[8,128]{1,0:T(8,128)} %bitcast_reduce_fusion.s_ref), custom_call_target="tpu_custom_call" | custom-call | tf_op jit(solution)/shard_map/gather_both/pallas_call | solution.py:180
  174.6 0.0 copy-start.3
  174.6 0.0 copy-start
  174.6 19.4 %fusion.x_ref = f32[1024,512]{1,0:T(8,128)} fusion(f32[1024,4096]{1,0:T(8,128)} %get-tuple-element.14, f32[4096,512]{1,0:T(8,128)} %get-tuple-element.15), kind=kOutput, calls=%fused_computation.5 | convolution fusion | flops 12884901888 | bytes 27262976 | tf_op jit(solution)/shard_map/dot_general | solution.py:206
  194.1 0.0 copy-done.3
  194.1 0.6 bitcast_reduce_fusion.2.s_ref
  194.7 67.5 %gather_cols.2 = (f32[4096,512]{1,0:T(8,128)}, f32[32,128]{1,0:T(8,128)}) custom-call(f32[1024,512]{1,0:T(8,128)} %fusion.x_ref, f32[8,128]{1,0:T(8,128)} %bitcast_reduce_fusion.2.s_ref), custom_call_target="tpu_custom_call" | custom-call | tf_op jit(solution)/shard_map/gather_cols/pallas_call | solution.py:194
  262.2 1.3 reduce_sum.38
  264.2 0.0 copy-done
  264.3 21.1 %subtract_multiply_fusion.x_ref = f32[1024,512]{1,0:T(8,128)} fusion(f32[1024,512]{1,0:T(8,128)S(1)} %copy-done, f32[1024,4096]{1,0:T(8,128)} %get-tuple-element.14, f32[4096,512]{1,0:T(8,128)} %get-tuple-element.18, f32[]{:T(128)S(6)} %mul.37, f32[]{:T(128)S(6)} %sqrt.3), kind=kOutput, calls=%fused_computation.2 | convolution fusion | flops 12886999040 | bytes 29360136 | tf_op jit(solution)/shard_map/dot_general | solution.py:206
  285.3 168.8 %gather_both.3 = (f32[1024,4096]{1,0:T(8,128)}, f32[4096,512]{1,0:T(8,128)}, f32[64,128]{1,0:T(8,128)}) custom-call(f32[1024,512]{1,0:T(8,128)} %subtract_multiply_fusion.x_ref, f32[8,128]{1,0:T(8,128)} %bitcast_reduce_fusion.s_ref), custom_call_target="tpu_custom_call" | custom-call | tf_op jit(solution)/shard_map/gather_both/pallas_call | solution.py:180
  454.1 0.0 copy-start.2
  454.1 0.0 copy-start.1
  454.1 19.5 %fusion.1.x_ref = f32[1024,512]{1,0:T(8,128)} fusion(f32[1024,4096]{1,0:T(8,128)} %get-tuple-element.19, f32[4096,512]{1,0:T(8,128)} %get-tuple-element.20), kind=kOutput, calls=%fused_computation.6 | convolution fusion | flops 12884901888 | bytes 27262976 | tf_op jit(solution)/shard_map/dot_general | solution.py:206
  473.7 0.0 copy-done.2
  473.7 0.6 bitcast_reduce_fusion.1.s_ref
  474.3 67.3 %gather_cols.3 = (f32[4096,512]{1,0:T(8,128)}, f32[32,128]{1,0:T(8,128)}) custom-call(f32[1024,512]{1,0:T(8,128)} %fusion.1.x_ref, f32[8,128]{1,0:T(8,128)} %bitcast_reduce_fusion.1.s_ref), custom_call_target="tpu_custom_call" | custom-call | tf_op jit(solution)/shard_map/gather_cols/pallas_call | solution.py:194
  541.6 0.0 copy-done.1
  541.6 19.6 %multiply_subtract_fusion = f32[1024,512]{1,0:T(8,128)} fusion(f32[1024,512]{1,0:T(8,128)S(1)} %copy-done.1, f32[1024,4096]{1,0:T(8,128)} %get-tuple-element.19, f32[4096,512]{1,0:T(8,128)} %get-tuple-element.22), kind=kOutput, calls=%fused_computation.1 | convolution fusion | flops 12886474752 | bytes 29360128 | tf_op jit(solution)/shard_map/dot_general | solution.py:206
Async XLA Ops:
  174.6 19.5 %copy-start.3 = (f32[64,128]{1,0:T(8,128)S(1)}, f32[64,128]{1,0:T(8,128)}, u32[]{:S(2)}) copy-start(f32[64,128]{1,0:T(8,128)} %get-tuple-element.16) | copy-start | bytes 98308
  174.6 89.6 %copy-start = (f32[1024,512]{1,0:T(8,128)S(1)}, f32[1024,512]{1,0:T(8,128)}, u32[]{:S(2)}) copy-start(f32[1024,512]{1,0:T(8,128)} %x_ref.1) | copy-start | bytes 6291460
  454.1 19.6 %copy-start.2 = (f32[64,128]{1,0:T(8,128)S(1)}, f32[64,128]{1,0:T(8,128)}, u32[]{:S(2)}) copy-start(f32[64,128]{1,0:T(8,128)} %get-tuple-element.21) | copy-start | bytes 98308
  454.1 87.4 %copy-start.1 = (f32[1024,512]{1,0:T(8,128)S(1)}, f32[1024,512]{1,0:T(8,128)}, u32[]{:S(2)}) copy-start(f32[1024,512]{1,0:T(8,128)} %subtract_multiply_fusion.x_ref) | copy-start | bytes 6291460
where the time goes:
time: 561 us
  Pallas kernels  475 us (85%)
  matrix products  79.6 us (14%)
    pallas_call x2, Pallas kernels, gather_both(): pl.pallas_call(functools.partial(both_kernel, row_n, col_n), out_shape=(j...  341 us
    pallas_call x2, Pallas kernels, gather_cols(): pl.pallas_call(functools.partial(cols_kernel, row_n), out_shape=(jax.Shap...  135 us
    dot_general x4, matrix products, dot(): jnp.dot(a, b, preferred_element_type=jnp.float32, precision=lax.Precision...  79.6 us

commit v1 on v0

v1 whole, which is shorter than its diff:
```python
import functools

import jax
import jax.numpy as jnp
from jax import lax
from jax.experimental import pallas as pl
from jax.experimental.pallas import tpu as pltpu
from jax.sharding import PartitionSpec as P

ITERS = 2
MESH = pl.DeviceIdType.MESH
ANY = pl.BlockSpec(memory_space=pl.ANY)
DMA = pltpu.SemaphoreType.DMA
F32, BF16 = jnp.float32, jnp.bfloat16


class Plan:
    def __init__(self, row_n, col_n, block):
        self.row_n, self.col_n = row_n, col_n
        self.h, self.w = block
        self.n = self.h * row_n
        self.ys, self.zs = row_n // 2, col_n // 2
        self.q = self.h // self.w
        self.halved = self.w % 256 == 0
        self.pw = self.w // 2 if self.halved else self.w
        self.pieces = max(2, self.h * self.pw // 32768)
        self.ph = self.h // self.pieces
        self.extra = self.pw // self.ph if self.halved else 0
        self.total = self.pieces + self.extra
        self.split = (self.w // self.ys) % 128 == 0
        self.cw = self.w // self.ys if self.split else self.w

    def locate(self):
        self.row, self.col = lax.axis_index("row"), lax.axis_index("col")
        self.core, self.y = lax.rem(self.row, 2), self.row // 2
        self.x, self.z = lax.rem(self.col, 2), self.col // 2

    def offset(self, row, col, piece):
        if not self.halved:
            return 0
        start = piece * self.ph
        upper = ((row * self.h + start) // self.w < col).astype(jnp.int32)
        return pl.multiple_of(self.pw * lax.rem(start // self.pw + upper, 2), self.pw)

    def place(self, row_block):
        swap = lax.rem(lax.rem(row_block, 2) + self.core, 2)
        return (swap * self.ys + row_block // 2) * self.h

    def is_mine(self, col):
        return lax.rem(col // self.q, 2) == self.core

    def is_diagonal(self, y, col):
        return col // self.q == 2 * y + self.core


def y_steps(plan):
    if plan.ys == 2:
        return ((0, 0), (1, 0))
    return ((0, 0),) + tuple((far, sign) for far in range(1, plan.ys) for sign in (1, -1))


def gather_kernel(plan, x_ref, stage, *rest):
    cross = rest[0] if plan.halved else None
    recv, send, cross_recv, cross_send, keep_sem = rest[-5:]
    plan.locate()
    row, col, core, x, y, z = plan.row, plan.col, plan.core, plan.x, plan.y, plan.z
    partner = row + 1 - 2 * core
    ways = [((row, col + 1 - 2 * x), True)]
    if plan.ys == 2:
        ways.append(((row + 2 - 4 * y, col), True))
    else:
        ways += [((row + 2, col), y < plan.ys - 1), ((row - 2, col), y > 0)]
    ways += [((row, col + 2), z < plan.zs - 1), ((row, col - 2), z > 0)]

    barrier = pltpu.get_barrier_semaphore()
    count = 1
    pl.semaphore_signal(barrier, inc=1, device_id=(partner, col), device_id_type=MESH)
    for target, there in ways:
        if there is True:
            count += 1
            pl.semaphore_signal(barrier, inc=1, device_id=target, device_id_type=MESH)
        else:
            count += there.astype(jnp.int32)

            @pl.when(there)
            def _():
                pl.semaphore_signal(barrier, inc=1, device_id=target, device_id_type=MESH)
    pl.semaphore_wait(barrier, count)

    def own(piece, extra):
        if extra:
            start = lax.rem(col, plan.q) * plan.w + (piece - plan.pieces) * plan.ph
            offset = plan.pw
        else:
            start, offset = piece * plan.ph, plan.offset(row, col, piece)
        return x_ref.at[pl.ds(pl.multiple_of(start, plan.ph), plan.ph), pl.ds(offset, plan.pw)]

    def link(act, way, src, sy, sc, piece):
        dst = stage.at[sy, sc, piece]
        at = sy * plan.col_n + sc
        getattr(pltpu.make_async_remote_copy(
            src_ref=dst if src is None else src, dst_ref=dst, send_sem=send.at[way, at, piece],
            recv_sem=recv.at[at, piece], device_id=ways[way][0], device_id_type=MESH), act)()

    def across(act, src, sy, sc, piece):
        if not plan.halved:
            return
        at = sy * plan.col_n + sc

        @pl.when((piece < plan.pieces) & (lax.rem(sc // plan.q, 2) != core))
        def _():
            getattr(pltpu.make_async_remote_copy(
                src_ref=stage.at[sy, sc, piece] if src is None else src, dst_ref=cross.at[sy, sc, piece],
                send_sem=cross_send.at[at, piece], recv_sem=cross_recv.at[at, piece],
                device_id=(partner, col), device_id_type=MESH), act)()

    def onward(act, src, sy, sc, piece, dx, dy, y_sign, dz, z_sign):
        z_last = piece < plan.pieces // 4
        y_first = lax.rem(piece, 2) == 1
        near = dz == 0
        z_done = jnp.logical_or(jnp.logical_not(z_last), near)

        def go(way, when):
            there = ways[way][1]

            @pl.when(when if there is True else when & there)
            def _():
                link(act, way, src, sy, sc, piece)

        if dx == 0:
            go(0, z_done if dy == 0 else z_done & y_first)
        y_open = z_done if dx == 0 else z_done & jnp.logical_not(y_first)
        if plan.ys == 2:
            if dy == 0:
                go(1, y_open)
        else:
            for way, sign in ((1, -1), (2, 1)):
                if dy == 0 or y_sign == sign:
                    go(way, y_open)
        first = len(ways) - 2
        for way, sign in ((first, -1), (first + 1, 1)):
            here = near | (z_sign == sign)
            go(way, here if dx == 0 and dy == 0 else here & z_last)

    def sweep(act):
        def own_step(extra):
            def step(piece, carry):
                src = own(piece, extra)
                onward(act, src, y, col, piece, 0, 0, 0, jnp.int32(0), 1)
                across(act, src, y, col, piece)
                copy = pltpu.make_async_copy(src, stage.at[y, col, piece], keep_sem.at[piece])
                copy.start() if act == "start" else copy.wait()
                return carry
            return step

        lax.fori_loop(0, plan.pieces, own_step(False), 0)
        if plan.extra:
            @pl.when(plan.is_diagonal(y, col))
            def _():
                lax.fori_loop(plan.pieces, plan.total, own_step(True), 0)

        def event(piece, far, dx, dy, y_sign, z_sign):
            dz = far - dx - dy
            sz = z + z_sign * dz
            sy = 1 - y if plan.ys == 2 and dy else y + y_sign * dy
            sc = 2 * sz + (1 - x if dx else x)
            there = (dz >= (0 if z_sign > 0 else 1)) & (sz >= 0) & (sz < plan.zs)
            if plan.ys != 2:
                there = there & (sy >= 0) & (sy < plan.ys)
            if plan.extra:
                there = there & ((piece < plan.pieces) | plan.is_diagonal(sy, sc))

            @pl.when(there)
            def _():
                if act == "start":
                    dst = stage.at[sy, sc, piece]
                    pltpu.make_async_remote_copy(
                        src_ref=dst, dst_ref=dst, send_sem=send.at[0, 0, 0],
                        recv_sem=recv.at[sy * plan.col_n + sc, piece],
                        device_id=ways[0][0], device_id_type=MESH).wait_recv()
                onward(act, None, sy, sc, piece, dx, dy, y_sign, dz, z_sign)
                across(act, None, sy, sc, piece)

        def round_(far, carry):
            def step(piece, carry):
                for dx in (0, 1):
                    for dy, y_sign in y_steps(plan):
                        for z_sign in (1, -1):
                            event(piece, far, dx, dy, y_sign, z_sign)
                return carry
            return lax.fori_loop(0, plan.total, step, carry)

        lax.fori_loop(1, plan.zs + plan.ys, round_, 0)

    sweep("start")
    sweep("wait_send" if True else None)
    if plan.halved:
        def last(at, carry):
            sy, sc = at // plan.col_n, lax.rem(at, plan.col_n)

            @pl.when(plan.is_mine(sc))
            def _():
                def step(piece, carry):
                    dst = cross.at[sy, sc, piece]
                    pltpu.make_async_remote_copy(
                        src_ref=dst, dst_ref=dst, send_sem=cross_send.at[0, 0], recv_sem=cross_recv.at[at, piece],
                        device_id=(partner, col), device_id_type=MESH).wait_recv()
                    return carry
                lax.fori_loop(0, plan.pieces, step, 0)
            return carry
        lax.fori_loop(0, plan.ys * plan.col_n, last, 0)


def gather(plan, x):
    full = (plan.ys, plan.col_n)
    shapes = [jax.ShapeDtypeStruct((*full, plan.total, plan.ph, plan.pw), F32)]
    if plan.halved:
        shapes.append(jax.ShapeDtypeStruct((*full, plan.pieces, plan.ph, plan.pw), F32))
    count = plan.ys * plan.col_n
    ways = 4 if plan.ys == 2 else 5
    return pl.pallas_call(
        functools.partial(gather_kernel, plan),
        out_shape=shapes, in_specs=[ANY], out_specs=[ANY] * len(shapes),
        scratch_shapes=[DMA((count, plan.total)), DMA((ways, count, plan.total)), DMA((count, plan.pieces)),
                        DMA((count, plan.pieces)), DMA((plan.total,))],
        compiler_params=pltpu.CompilerParams(collective_id=0, has_side_effects=True),
        name="gather",
    )(x)


STEPS = 8


def weights(step):
    def pick(table, other):
        value = jnp.float32(other)
        for at, entry in table:
            value = jnp.where(step == at, jnp.float32(entry), value)
        return value
    return (pick(((1, 1.5), (7, 1.5)), 0.0), pick(((4, 1.5), (7, -0.75)), 0.0),
            pick(((1, -0.5), (4, -0.5), (7, 0.25)), 1.0))


def apply_kernel(plan, stage, *rest):
    if plan.halved:
        cross, rest = rest[0], rest[1:]
    (out, high, low, own_high, own_low, peer_high, peer_low, panel, peer, first, second, loaded, squares, peer_squares,
     scale, load_sem, panel_send, panel_recv, square_sems, out_local, out_send, out_recv) = rest
    plan.locate()
    row, col, core, x, y, z = plan.row, plan.col, plan.core, plan.x, plan.y, plan.z
    h, w, q, ph, pw, half, cw = plan.h, plan.w, plan.q, plan.ph, plan.pw, plan.n // 2, plan.cw
    partner = (row + 1 - 2 * core, col)

    barrier = pltpu.get_barrier_semaphore()
    pl.semaphore_signal(barrier, inc=1, device_id=partner, device_id_type=MESH)
    if plan.split:
        for far in range(1, plan.ys):
            pl.semaphore_signal(barrier, inc=1, device_id=(2 * lax.rem(y + far, plan.ys) + core, col), device_id_type=MESH)
    pl.semaphore_wait(barrier, plan.ys if plan.split else 1)

    def put(tile, at, to):
        top = tile.astype(BF16)
        rest = (tile - top.astype(F32)).astype(BF16)
        rows = pl.ds(pl.multiple_of(at, tile.shape[0]), tile.shape[0])
        cols = pl.ds(pl.multiple_of(to, tile.shape[1]), tile.shape[1])
        high[rows, cols] = top
        low[rows, cols] = rest
        both = tile * tile
        squares[...] += jnp.sum(both.reshape(tile.shape[0] // 8, 8, tile.shape[1] // 128, 128), axis=(0, 2))

    def put_direct(tile, sy, sc, piece):
        put(tile, sy * h + piece * ph, plan.place(sc // q) + lax.rem(sc, q) * w + plan.offset(2 * sy + core, sc, piece))

    def put_turned(tile, sy, core_from, sc, piece):
        source = 2 * sy + core_from
        at = (sc // q // 2) * h + lax.rem(sc, q) * w + plan.offset(source, sc, piece)
        put(tile.T, at, plan.place(source) + piece * ph)

    squares[...] = jnp.zeros_like(squares)

    def streamed(count, source, use):
        def fetch(at):
            slot = lax.rem(at, 2)
            return pltpu.make_async_copy(source(at), loaded.at[slot], load_sem.at[slot])
        fetch(0).start()

        def step(at, carry):
            @pl.when(at + 1 < count)
            def _():
                fetch(at + 1).start()
            fetch(at).wait()
            use(at, loaded.at[lax.rem(at, 2)])
            return carry
        lax.fori_loop(0, count, step, 0)

    def stage_of(at):
        return stage.at[at // plan.col_n, lax.rem(at, plan.col_n), pl.ds(0, plan.pieces)]

    def use_stage(at, ref):
        sy, sc = at // plan.col_n, lax.rem(at, plan.col_n)

        def step(piece, carry):
            put_direct(ref[piece], sy, sc, piece)
            if plan.halved:
                block = ((2 * sy + core) * h + piece * ph) // w

                @pl.when(plan.is_mine(sc) & (block != sc))
                def _():
                    put_turned(ref[piece], sy, core, sc, piece)
            return carry
        lax.fori_loop(0, plan.pieces, step, 0)

    streamed(plan.ys * plan.col_n, stage_of, use_stage)

    if plan.halved:
        def mine(at):
            u = lax.rem(at, plan.col_n // 2)
            return at // (plan.col_n // 2), (2 * (u // q) + core) * q + lax.rem(u, q)

        def use_cross(at, ref):
            sy, sc = mine(at)

            def step(piece, carry):
                put_turned(ref[piece], sy, 1 - core, sc, piece)
                return carry
            lax.fori_loop(0, plan.pieces, step, 0)

        def cross_of(at):
            sy, sc = mine(at)
            return cross.at[sy, sc]

        streamed(plan.ys * plan.col_n // 2, cross_of, use_cross)

        def diagonal(at, carry):
            sy = at // q
            sc = q * (2 * sy + core) + lax.rem(at, q)
            some = loaded.at[0, pl.ds(0, plan.extra)]
            copy = pltpu.make_async_copy(stage.at[sy, sc, pl.ds(plan.pieces, plan.extra)], some, load_sem.at[0])
            copy.start()
            copy.wait()
            corner = sy * h + lax.rem(sc, q) * w
            base = plan.place(sc // q) + lax.rem(sc, q) * w
            for e in range(plan.extra):
                tile = loaded[0, e]
                put(tile, corner + e * ph, base + pw)
                put(tile.T, corner + pw, base + e * ph)
            return carry
        lax.fori_loop(0, plan.ys * q, diagonal, 0)

    share = pltpu.make_async_remote_copy(src_ref=squares, dst_ref=peer_squares, send_sem=square_sems.at[0],
                                         recv_sem=square_sems.at[1], device_id=partner, device_id_type=MESH)
    share.start()
    share.wait()
    total = jnp.sum(jnp.sum(squares[...] + peer_squares[...], axis=0, keepdims=True), axis=1, keepdims=True)
    scale[...] = jnp.broadcast_to(jnp.sqrt(plan.n / total), scale.shape)

    def send(slot, tile):
        rows = pl.ds(pl.multiple_of(tile * h, h), h)
        return pltpu.make_async_remote_copy(
            src_ref=panel.at[slot, rows], dst_ref=peer.at[slot, rows], send_sem=panel_send.at[slot, tile],
            recv_sem=panel_recv.at[slot, tile], device_id=partner, device_id_type=MESH)

    def parts(value):
        top = value.astype(BF16)
        return top, (value - top.astype(F32)).astype(BF16)

    start = plan.place(col // q) + lax.rem(col, q) * w + (y * cw if plan.split else 0)
    mine_cols = pl.ds(pl.multiple_of(start, cw), cw)

    def begin(tile, carry):
        rows = pl.ds(pl.multiple_of(tile * h, h), h)
        value = scale[0:1, 0:1] * (high[rows, mine_cols].astype(F32) + low[rows, mine_cols].astype(F32))
        first[rows, :] = value
        second[rows, :] = value
        panel[0, rows] = value
        own_high[rows, :], own_low[rows, :] = parts(value)
        send(0, tile).start()
        return carry
    lax.fori_loop(0, plan.ys, begin, 0)

    def product(rows, cols, b_high, b_low):
        a_high, a_low = high[rows, cols], low[rows, cols]
        top = b_high[...]
        acc = jnp.dot(a_high, top, preferred_element_type=F32)
        acc += jnp.dot(a_high, b_low[...], preferred_element_type=F32)
        return acc + jnp.dot(a_low, top, preferred_element_type=F32)

    def deliver(act):
        for far in range(1, plan.ys):
            to = lax.rem(y + far, plan.ys)
            copy = pltpu.make_async_remote_copy(
                src_ref=panel.at[STEPS % 2, pl.ds(pl.multiple_of(to * h, h), h)],
                dst_ref=out.at[:, pl.ds(pl.multiple_of(y * cw, cw), cw)],
                send_sem=out_send.at[far - 1], recv_sem=out_recv.at[far - 1],
                device_id=(2 * to + core, col), device_id_type=MESH)
            getattr(copy, act)()

    def step_(step, carry):
        now, later = lax.rem(step, 2), lax.rem(step + 1, 2)

        @pl.when(step > 0)
        def _():
            for tile in range(plan.ys):
                send(later, tile).wait_send()

        def near(tile, carry):
            rows = pl.ds(pl.multiple_of(tile * h, h), h)
            panel[later, rows] = product(rows, slice(0, half), own_high, own_low)
            return carry
        lax.fori_loop(0, plan.ys, near, 0)

        for tile in range(plan.ys):
            send(now, tile).wait_recv()
        peer_high[...], peer_low[...] = parts(peer[now])
        a, b, c = weights(step)

        def far(at, carry):
            tile = lax.rem(y + 1 + at, plan.ys)
            rows = pl.ds(pl.multiple_of(tile * h, h), h)
            value = scale[0:1, 0:1] * (panel[later, rows] + product(rows, slice(half, 2 * half), peer_high, peer_low))
            value = a * first[rows, :] + b * second[rows, :] + c * value
            panel[later, rows] = value
            own_high[rows, :], own_low[rows, :] = parts(value)

            @pl.when(step == 1)
            def _():
                first[rows, :] = value

            @pl.when((step == 2) | (step == 5))
            def _():
                second[rows, :] = value

            @pl.when(step < STEPS - 1)
            def _():
                send(later, tile).start()
            return carry
        lax.fori_loop(0, plan.ys, far, 0)
        return carry
    lax.fori_loop(0, STEPS, step_, 0)
    for tile in range(plan.ys):
        send((STEPS - 1) % 2, tile).wait_send()

    local = pltpu.make_async_copy(
        panel.at[STEPS % 2, pl.ds(pl.multiple_of(y * h, h), h)],
        out.at[:, pl.ds(pl.multiple_of(y * cw if plan.split else 0, cw), cw)], out_local)
    local.start()
    if plan.split:
        deliver("start")
        deliver("wait")
    local.wait()


def apply(plan, staged):
    h, half, cw = plan.h, plan.n // 2, plan.cw
    vmem = pltpu.VMEM
    return pl.pallas_call(
        functools.partial(apply_kernel, plan),
        out_shape=jax.ShapeDtypeStruct((h, plan.w), F32), in_specs=[ANY] * len(staged), out_specs=ANY,
        scratch_shapes=[vmem((half, plan.n), BF16)] * 2 + [vmem((half, cw), BF16)] * 4
        + [vmem((2, half, cw), F32)] * 2 + [vmem((half, cw), F32)] * 2
        + [vmem((2, plan.pieces, plan.ph, plan.pw), F32), vmem((8, 128), F32), vmem((8, 128), F32), vmem((8, 128), F32),
           DMA((2,)), DMA((2, plan.ys)), DMA((2, plan.ys)), DMA((2,)), DMA(()), DMA((plan.ys - 1,)), DMA((plan.ys - 1,))],
        compiler_params=pltpu.CompilerParams(collective_id=1, has_side_effects=True, vmem_limit_bytes=63 * 2**20),
        name="apply",
    )(*staged)


def shards(row_n, col_n, matrix):
    plan = Plan(row_n, col_n, matrix.shape)
    return apply(plan, gather(plan, matrix))


def solution(mesh):
    body = functools.partial(shards, mesh.shape["row"], mesh.shape["col"])
    return jax.shard_map(body, mesh=mesh, in_specs=(P("row", "col"),), out_specs=P("row", "col"), check_vma=False)
```

time: 561 us -> 351 us (0.63)
  Pallas kernels: 475 us -> 348 us
  matrix products: 79.6 us -> 0 us
    pallas_call x4 -> x2, Pallas kernels: 475 us -> 348 us  [the longest x1 193 us: apply(): pl.pallas_call(functools.partial(apply_kernel, plan), out_shape=jax.Shape...]
    dot_general x4 -> x0, matrix products: 79.6 us -> none  [dot(): jnp.dot(a, b, preferred_element_type=jnp.float32, precision=lax.Precision...]
where the time goes in v1:
time: 351 us
  Pallas kernels  348 us (99%)
    pallas_call x1, Pallas kernels, apply(): pl.pallas_call(functools.partial(apply_kernel, plan), out_shape=jax.Shape...  193 us
    pallas_call x1, Pallas kernels, gather(): pl.pallas_call(functools.partial(gather_kernel, plan), out_shape=shapes,...  155 us

profile of v1, /device:TPU:0, one launch (start us, length us, event | category | flops | bytes accessed | tf_op | source)
XLA Modules:
  0.0 350.9 jit_solution(7120289461328497480)
XLA Ops:
  0.0 154.9 %gather.1 = (f32[2,8,10,128,256]{4,3,2,1,0:T(8,128)}, f32[2,8,8,128,256]{4,3,2,1,0:T(8,128)}) custom-call(f32[1024,512]{1,0:T(8,128)} %x_ref.1), custom_call_target="tpu_custom_call" | custom-call | tf_op jit(solution)/shard_map/gather/pallas_call | solution.py:221
  154.9 192.9 %apply.1 = f32[1024,512]{1,0:T(8,128)} custom-call(f32[2,8,10,128,256]{4,3,2,1,0:T(8,128)} %get-tuple-element.7.stage, f32[2,8,8,128,256]{4,3,2,1,0:T(8,128)} %get-tuple-element.8.rest_0_), custom_call_target="tpu_custom_call" | custom-call | tf_op jit(solution)/shard_map/apply/pallas_call | solution.py:456
  347.8 3.1 copy.3

commit v2 on v1

v2 whole, which is shorter than its diff:
```python
import functools

import jax
import jax.numpy as jnp
from jax import lax
from jax.experimental import pallas as pl
from jax.experimental.pallas import tpu as pltpu
from jax.sharding import PartitionSpec as P

ITERS = 2
MESH = pl.DeviceIdType.MESH
ANY = pl.BlockSpec(memory_space=pl.ANY)
DMA = pltpu.SemaphoreType.DMA
F32, BF16 = jnp.float32, jnp.bfloat16


class Plan:
    def __init__(self, row_n, col_n, block):
        self.row_n, self.col_n = row_n, col_n
        self.h, self.w = block
        self.n = self.h * row_n
        self.ys, self.zs = row_n // 2, col_n // 2
        self.q = self.h // self.w
        self.halved = self.w % 256 == 0
        self.pw = self.w // 2 if self.halved else self.w
        self.pieces = max(2, self.h * self.pw // 32768)
        self.ph = self.h // self.pieces
        self.extra = self.pw // self.ph if self.halved else 0
        self.total = self.pieces + self.extra
        self.split = (self.w // self.ys) % 128 == 0
        self.cw = self.w // self.ys if self.split else self.w

    def locate(self):
        self.row, self.col = lax.axis_index("row"), lax.axis_index("col")
        self.core, self.y = lax.rem(self.row, 2), self.row // 2
        self.x, self.z = lax.rem(self.col, 2), self.col // 2

    def offset(self, row, col, piece):
        if not self.halved:
            return 0
        start = piece * self.ph
        upper = ((row * self.h + start) // self.w < col).astype(jnp.int32)
        return pl.multiple_of(self.pw * lax.rem(start // self.pw + upper, 2), self.pw)

    def place(self, row_block):
        swap = lax.rem(lax.rem(row_block, 2) + self.core, 2)
        return (swap * self.ys + row_block // 2) * self.h

    def is_mine(self, col):
        return lax.rem(col // self.q, 2) == self.core

    def is_diagonal(self, y, col):
        return col // self.q == 2 * y + self.core


def places(plan):
    ys = ((0, 0), (1, 0)) if plan.ys == 2 else ((0, 0),) + tuple(
        (far, sign) for far in range(1, plan.ys) for sign in (1, -1))
    return [(dx, dy, y_sign, z_sign) for dx in (0, 1) for dy, y_sign in ys for z_sign in (1, -1)]


class Gather:
    def __init__(self, plan, x_ref, stage, cross, put, tiles, turned, sems):
        self.plan, self.x_ref, self.stage, self.cross, self.put = plan, x_ref, stage, cross, put
        self.tiles, self.turned = tiles, turned
        self.recv, self.send, self.cross_recv, self.cross_send, self.tile_sem, self.turned_sem = sems
        row, col, x, y, z = plan.row, plan.col, plan.x, plan.y, plan.z
        self.partner = (row + 1 - 2 * plan.core, col)
        self.ways = [((row, col + 1 - 2 * x), True)]
        if plan.ys == 2:
            self.ways.append(((row + 2 - 4 * y, col), True))
        else:
            self.ways += [((row - 2, col), y > 0), ((row + 2, col), y < plan.ys - 1)]
        self.ways += [((row, col - 2), z > 0), ((row, col + 2), z < plan.zs - 1)]

    def greet(self):
        plan, barrier = self.plan, pltpu.get_barrier_semaphore()
        count = 1
        pl.semaphore_signal(barrier, inc=1, device_id=self.partner, device_id_type=MESH)
        for target, there in self.ways:
            if there is True:
                count += 1
                pl.semaphore_signal(barrier, inc=1, device_id=target, device_id_type=MESH)
            else:
                count += there.astype(jnp.int32)

                @pl.when(there)
                def _():
                    pl.semaphore_signal(barrier, inc=1, device_id=target, device_id_type=MESH)
        if plan.split and plan.ys > 2:
            count += plan.ys - 1
            for far in range(1, plan.ys):
                target = (2 * lax.rem(plan.y + far, plan.ys) + plan.core, plan.col)
                pl.semaphore_signal(barrier, inc=1, device_id=target, device_id_type=MESH)
        pl.semaphore_wait(barrier, count)

    def own(self, piece, extra=False):
        plan = self.plan
        if extra:
            start = lax.rem(plan.col, plan.q) * plan.w + (piece - plan.pieces) * plan.ph
            offset = plan.pw
        else:
            start, offset = piece * plan.ph, plan.offset(plan.row, plan.col, piece)
        return self.x_ref.at[pl.ds(pl.multiple_of(start, plan.ph), plan.ph), pl.ds(offset, plan.pw)]

    def link(self, act, way, src, sy, sc, piece):
        dst, at = self.stage.at[sy, sc, piece], sy * self.plan.col_n + sc
        getattr(pltpu.make_async_remote_copy(
            src_ref=dst if src is None else src, dst_ref=dst, send_sem=self.send.at[way, at, piece],
            recv_sem=self.recv.at[at, piece], device_id=self.ways[way][0], device_id_type=MESH), act)()

    def across(self, act, src, sy, sc, piece):
        plan, at = self.plan, sy * self.plan.col_n + sc
        if not plan.halved:
            return

        @pl.when((piece < plan.pieces) & jnp.logical_not(plan.is_mine(sc)))
        def _():
            getattr(pltpu.make_async_remote_copy(
                src_ref=self.stage.at[sy, sc, piece] if src is None else src, dst_ref=self.cross.at[sy, sc, piece],
                send_sem=self.cross_send.at[at, piece], recv_sem=self.cross_recv.at[at, piece],
                device_id=self.partner, device_id_type=MESH), act)()

    def onward(self, act, src, where, piece, spot):
        plan = self.plan
        dx, dy, y_sign, z_sign = where
        sy, sc, dz, _ = spot
        z_last = piece < plan.pieces // 4
        y_first = lax.rem(piece, 2) == 1
        near = dz == 0
        z_done = jnp.logical_or(jnp.logical_not(z_last), near)

        def go(way, when):
            there = self.ways[way][1]

            @pl.when(when if there is True else when & there)
            def _():
                self.link(act, way, src, sy, sc, piece)

        first = len(self.ways) - 2
        for way, sign in ((first, 1), (first + 1, -1)):
            here = near | (z_sign == sign)
            go(way, here if dx == 0 and dy == 0 else here & z_last)
        if dx == 0:
            go(0, z_done if dy == 0 else z_done & y_first)
        y_open = z_done if dx == 0 else z_done & jnp.logical_not(y_first)
        if plan.ys == 2:
            if dy == 0:
                go(1, y_open)
        else:
            for way, sign in ((1, 1), (2, -1)):
                if dy == 0 or y_sign == sign:
                    go(way, y_open)

    def spot(self, where, far, piece):
        plan = self.plan
        dx, dy, y_sign, z_sign = where
        dz = far - dx - dy
        sz = plan.z + z_sign * dz
        sy = 1 - plan.y if plan.ys == 2 and dy else plan.y + y_sign * dy
        sc = 2 * sz + (1 - plan.x if dx else plan.x)
        there = (dz >= (0 if z_sign > 0 else 1)) & (sz >= 0) & (sz < plan.zs)
        if plan.ys != 2:
            there = there & (sy >= 0) & (sy < plan.ys)
        if plan.extra:
            there = there & ((piece < plan.pieces) | plan.is_diagonal(sy, sc))
        return sy, sc, dz, there

    def begin(self):
        plan = self.plan
        here = (0, 0, 0, 1)

        def step(extra):
            def start(piece, carry):
                src = self.own(piece, extra)
                self.onward("start", src, here, piece, (plan.y, plan.col, jnp.int32(0), None))
                self.across("start", src, plan.y, plan.col, piece)
                return carry
            return start
        lax.fori_loop(0, plan.pieces, step(False), 0)
        if plan.extra:
            @pl.when(plan.is_diagonal(plan.y, plan.col))
            def _():
                lax.fori_loop(plan.pieces, plan.total, step(True), 0)

    def wait_arrival(self, sy, sc, piece):
        dst = self.stage.at[sy, sc, piece]
        pltpu.make_async_remote_copy(
            src_ref=dst, dst_ref=dst, send_sem=self.send.at[0, 0, 0], recv_sem=self.recv.at[sy * self.plan.col_n + sc, piece],
            device_id=self.ways[0][0], device_id_type=MESH).wait_recv()

    def wait_cross(self, sy, sc, piece):
        dst = self.cross.at[sy, sc, piece]
        pltpu.make_async_remote_copy(
            src_ref=dst, dst_ref=dst, send_sem=self.cross_send.at[0, 0],
            recv_sem=self.cross_recv.at[sy * self.plan.col_n + sc, piece],
            device_id=self.partner, device_id_type=MESH).wait_recv()

    def lay(self, tile, sy, sc, piece):
        plan = self.plan
        h, w, q, ph, pw = plan.h, plan.w, plan.q, plan.ph, plan.pw
        inner = lax.rem(sc, q) * w
        row, col = piece * ph, inner + plan.offset(2 * sy + plan.core, sc, piece)
        if plan.extra:
            normal, past = piece < plan.pieces, (piece - plan.pieces) * ph
            row, col = jnp.where(normal, row, inner + past), jnp.where(normal, col, inner + pw)
        base = plan.place(sc // q)
        self.put(tile[...], sy * h + row, base + col)
        if plan.halved:
            block = ((2 * sy + plan.core) * h + row) // w

            @pl.when((plan.is_mine(sc) & (block != sc)) | jnp.logical_not(normal))
            def _():
                self.put(tile[...].T, (sc // q // 2) * h + col, sy * h + row)

    def lay_turned(self, tile, sy, sc, piece):
        plan = self.plan
        source = 2 * sy + 1 - plan.core
        at = (sc // plan.q // 2) * plan.h + lax.rem(sc, plan.q) * plan.w + plan.offset(source, sc, piece)
        self.put(tile[...].T, at, plan.place(source) + piece * plan.ph)

    def run(self):
        plan = self.plan
        wheres = places(plan)

        def fetch(act, src, slot, e):
            getattr(pltpu.make_async_copy(src, self.tiles.at[slot, e], self.tile_sem.at[slot, e]), act)()

        def fetch_turned(act, sy, sc, piece, slot, e):
            getattr(pltpu.make_async_copy(
                self.cross.at[sy, sc, piece], self.turned.at[slot, e], self.turned_sem.at[slot, e]), act)()

        def turn(where, far, piece):
            sy, sc, dz, there = self.spot(where, far, piece)
            return sy, sc, there & (piece < plan.pieces) & plan.is_mine(sc)

        def one(far, piece, e, where):
            slot = lax.rem(far * plan.total + piece, 2)
            spot = self.spot(where, far, piece)
            sy, sc, _, there = spot

            @pl.when(there & (far > 0))
            def _():
                self.wait_arrival(sy, sc, piece)
                self.onward("start", None, where, piece, spot)
                self.across("start", None, sy, sc, piece)

            wrap = (piece == 0).astype(jnp.int32)
            old_far, old_piece = far - wrap, piece - 1 + wrap * plan.total
            oy, oc, _, old = self.spot(where, old_far, old_piece)

            @pl.when(old)
            def _():
                fetch("wait", self.stage.at[oy, oc, old_piece], 1 - slot, e)
                self.lay(self.tiles.at[1 - slot, e], oy, oc, old_piece)

            @pl.when(there & (far > 0))
            def _():
                fetch("start", self.stage.at[sy, sc, piece], slot, e)
            if where == (0, 0, 0, 1):
                @pl.when(there & (far == 0) & (piece < plan.pieces))
                def _():
                    fetch("start", self.own(piece), slot, e)
                if plan.extra:
                    @pl.when(there & (far == 0) & (piece >= plan.pieces))
                    def _():
                        fetch("start", self.own(piece, True), slot, e)

            if plan.halved:
                ty, tc, old_turn = turn(where, old_far - 1, old_piece)

                @pl.when(old_turn)
                def _():
                    fetch_turned("wait", ty, tc, old_piece, 1 - slot, e)
                    self.lay_turned(self.turned.at[1 - slot, e], ty, tc, old_piece)
                uy, uc, new_turn = turn(where, far - 1, piece)

                @pl.when(new_turn)
                def _():
                    self.wait_cross(uy, uc, piece)
                    fetch_turned("start", uy, uc, piece, slot, e)
                vy, vc, _, sent = self.spot(where, far - 1, piece)

                @pl.when(sent)
                def _():
                    self.across("wait_send", None, vy, vc, piece)
            done = self.spot(where, far - 2, piece)

            @pl.when(done[3])
            def _():
                self.onward("wait_send", None, where, piece, done)

        def round_(far, carry):
            def step(piece, carry):
                for e, where in enumerate(wheres):
                    one(far, piece, e, where)
                return carry
            return lax.fori_loop(0, plan.total, step, carry)

        lax.fori_loop(0, plan.zs + plan.ys + 1, round_, 0)


STEPS = 8


def weights(step):
    def pick(table, other):
        value = jnp.float32(other)
        for at, entry in table:
            value = jnp.where(step == at, jnp.float32(entry), value)
        return value
    return pick(((1, 1.5),), 0.0), pick(((4, 1.5),), 0.0), pick(((1, -0.5), (4, -0.5)), 1.0)


def sign_kernel(plan, x_ref, *rest):
    if plan.halved:
        out, stage, cross = rest[:3]
        rest = rest[3:]
    else:
        out, stage = rest[:2]
        cross, rest = None, rest[2:]
    (high, low, own_high, own_low, peer_high, peer_low, panel, peer, first, second, tiles, turned, squares, peer_squares,
     scale, recv, send_sem, cross_recv, cross_send, tile_sem, turned_sem, panel_send, panel_recv, square_sems, out_local,
     out_send, out_recv) = rest
    plan.locate()
    col, core, y = plan.col, plan.core, plan.y
    h, w, q, half, cw = plan.h, plan.w, plan.q, plan.n // 2, plan.cw

    def put(tile, at, to):
        top = tile.astype(BF16)
        rest = (tile - top.astype(F32)).astype(BF16)
        rows = pl.ds(pl.multiple_of(at, tile.shape[0]), tile.shape[0])
        cols = pl.ds(pl.multiple_of(to, tile.shape[1]), tile.shape[1])
        high[rows, cols] = top
        low[rows, cols] = rest
        both = tile * tile
        squares[...] += jnp.sum(both.reshape(tile.shape[0] // 8, 8, tile.shape[1] // 128, 128), axis=(0, 2))

    gather = Gather(plan, x_ref, stage, cross, put, tiles, turned,
                    (recv, send_sem, cross_recv, cross_send, tile_sem, turned_sem))
    gather.greet()
    gather.begin()
    squares[...] = jnp.zeros_like(squares)
    gather.run()
    partner = gather.partner

    share = pltpu.make_async_remote_copy(src_ref=squares, dst_ref=peer_squares, send_sem=square_sems.at[0],
                                         recv_sem=square_sems.at[1], device_id=partner, device_id_type=MESH)
    share.start()
    share.wait()
    total = jnp.sum(jnp.sum(squares[...] + peer_squares[...], axis=0, keepdims=True), axis=1, keepdims=True)
    scale[...] = jnp.broadcast_to(jnp.sqrt(plan.n / total), scale.shape)

    def rows_of(tile):
        return pl.ds(pl.multiple_of(tile * h, h), h)

    def send(slot, tile):
        rows = rows_of(tile)
        return pltpu.make_async_remote_copy(
            src_ref=panel.at[slot, rows], dst_ref=peer.at[slot, rows], send_sem=panel_send.at[slot, tile],
            recv_sem=panel_recv.at[slot, tile], device_id=partner, device_id_type=MESH)

    def parts(value):
        top = value.astype(BF16)
        return top, (value - top.astype(F32)).astype(BF16)

    start = plan.place(col // q) + lax.rem(col, q) * w + (y * cw if plan.split else 0)
    mine_cols = pl.ds(pl.multiple_of(start, cw), cw)

    def begin(tile, carry):
        rows = rows_of(tile)
        value = scale[0:1, 0:1] * (high[rows, mine_cols].astype(F32) + low[rows, mine_cols].astype(F32))
        first[rows, :] = value
        second[rows, :] = value
        panel[0, rows] = value
        own_high[rows, :], own_low[rows, :] = parts(value)
        send(0, tile).start()
        return carry
    lax.fori_loop(0, plan.ys, begin, 0)

    def product(rows, cols, b_high, b_low):
        a_high, a_low = high[rows, cols], low[rows, cols]
        top = b_high[...]
        acc = jnp.dot(a_high, top, preferred_element_type=F32)
        acc += jnp.dot(a_high, b_low[...], preferred_element_type=F32)
        return acc + jnp.dot(a_low, top, preferred_element_type=F32)

    def near(slot, tile):
        rows = rows_of(tile)
        panel[slot, rows] = product(rows, slice(0, half), own_high, own_low)

    def far(slot, rows):
        return scale[0:1, 0:1] * (panel[slot, rows] + product(rows, slice(half, 2 * half), peer_high, peer_low))

    def meet(slot):
        for tile in range(plan.ys):
            send(slot, tile).wait_recv()
        peer_high[...], peer_low[...] = parts(peer[slot])

    def sent(slot):
        for tile in range(plan.ys):
            send(slot, tile).wait_send()

    def step_(step, carry):
        now, later = lax.rem(step, 2), lax.rem(step + 1, 2)

        @pl.when(step > 0)
        def _():
            sent(later)

        def near_(tile, carry):
            near(later, tile)
            return carry
        lax.fori_loop(0, plan.ys, near_, 0)
        meet(now)
        a, b, c = weights(step)

        def far_(tile, carry):
            rows = rows_of(tile)
            value = a * first[rows, :] + b * second[rows, :] + c * far(later, rows)
            panel[later, rows] = value
            own_high[rows, :], own_low[rows, :] = parts(value)
            send(later, tile).start()

            @pl.when(step == 1)
            def _():
                first[rows, :] = value

            @pl.when((step == 2) | (step == 5))
            def _():
                second[rows, :] = value
            return carry
        lax.fori_loop(0, plan.ys, far_, 0)
        return carry
    lax.fori_loop(0, STEPS - 1, step_, 0)

    now, later = (STEPS - 1) % 2, STEPS % 2
    chunk = h // CHUNKS
    sent(later)

    def deliver(tile, far, part):
        return pltpu.make_async_remote_copy(
            src_ref=panel.at[later, pl.ds(pl.multiple_of(tile * h + part * chunk, chunk), chunk)],
            dst_ref=out.at[pl.ds(pl.multiple_of(part * chunk, chunk), chunk), pl.ds(pl.multiple_of(y * cw, cw), cw)],
            send_sem=out_send.at[far, part], recv_sem=out_recv.at[far, part],
            device_id=(2 * tile + core, col), device_id_type=MESH)

    def result(far_off, carry):
        tile = lax.rem(y + 1 + far_off, plan.ys)
        near(later, tile)

        @pl.when(far_off == 0)
        def _():
            meet(now)

        def piece(part, carry):
            rows = pl.ds(pl.multiple_of(tile * h + part * chunk, chunk), chunk)
            panel[later, rows] = 1.5 * first[rows, :] - 0.75 * second[rows, :] + 0.25 * far(later, rows)
            if plan.split:
                @pl.when(far_off < plan.ys - 1)
                def _():
                    deliver(tile, far_off, part).start()
            return carry
        lax.fori_loop(0, CHUNKS, piece, 0)
        return carry
    lax.fori_loop(0, plan.ys, result, 0)

    local = pltpu.make_async_copy(
        panel.at[later, rows_of(y)],
        out.at[:, pl.ds(pl.multiple_of(y * cw if plan.split else 0, cw), cw)], out_local)
    local.start()
    sent(now)
    if plan.split:
        for far_off in range(plan.ys - 1):
            for part in range(CHUNKS):
                deliver(lax.rem(y + 1 + far_off, plan.ys), far_off, part).wait()
    local.wait()


CHUNKS = 2


def shards(row_n, col_n, matrix):
    plan = Plan(row_n, col_n, matrix.shape)
    h, half, cw = plan.h, plan.n // 2, plan.cw
    vmem = pltpu.VMEM
    full, count = (plan.ys, plan.col_n), plan.ys * plan.col_n
    shapes = [jax.ShapeDtypeStruct((h, plan.w), F32),
              jax.ShapeDtypeStruct((*full, plan.total, plan.ph, plan.pw), F32)]
    if plan.halved:
        shapes.append(jax.ShapeDtypeStruct((*full, plan.pieces, plan.ph, plan.pw), F32))
    spots = len(places(plan))
    turned = (2, spots, plan.ph, plan.pw) if plan.halved else (8, 128)
    return pl.pallas_call(
        functools.partial(sign_kernel, plan),
        out_shape=shapes, in_specs=[ANY], out_specs=[ANY] * len(shapes),
        scratch_shapes=[vmem((half, plan.n), BF16)] * 2 + [vmem((half, cw), BF16)] * 4
        + [vmem((2, half, cw), F32)] * 2 + [vmem((half, cw), F32)] * 2
        + [vmem((2, spots, plan.ph, plan.pw), F32), vmem(turned, F32)] + [vmem((8, 128), F32)] * 3
        + [DMA((count, plan.total)), DMA((4 if plan.ys == 2 else 5, count, plan.total)), DMA((count, plan.pieces)),
           DMA((count, plan.pieces)), DMA((2, spots)), DMA((2, spots))]
        + [DMA((2, plan.ys)), DMA((2, plan.ys)), DMA((2,)), DMA(()), DMA((plan.ys - 1, CHUNKS)),
           DMA((plan.ys - 1, CHUNKS))],
        compiler_params=pltpu.CompilerParams(collective_id=0, has_side_effects=True, vmem_limit_bytes=63 * 2**20),
        name="sign",
    )(matrix)[0]


def solution(mesh):
    body = functools.partial(shards, mesh.shape["row"], mesh.shape["col"])
    return jax.shard_map(body, mesh=mesh, in_specs=(P("row", "col"),), out_specs=P("row", "col"), check_vma=False)
```

time: 351 us -> 311 us (0.89)
  Pallas kernels: 348 us -> 307 us
    pallas_call x2 -> x1, Pallas kernels: 348 us -> 307 us  [shards(): pl.pallas_call(functools.partial(sign_kernel, plan), out_shape=shapes, in...]
where the time goes in v2:
time: 311 us; the launch traced here: 310 us
  Pallas kernels  307 us (99%)
    pallas_call x1, Pallas kernels, shards(): pl.pallas_call(functools.partial(sign_kernel, plan), out_shape=shapes, in...  307 us

profile of v2, /device:TPU:0, one launch (start us, length us, event | category | flops | bytes accessed | tf_op | source)
XLA Modules:
  0.0 310.4 jit_solution(6180272268090450334)
XLA Ops:
  0.0 307.3 %sign.1 = (f32[1024,512]{1,0:T(8,128)}, f32[2,8,10,128,256]{4,3,2,1,0:T(8,128)}, f32[2,8,8,128,256]{4,3,2,1,0:T(8,128)}) custom-call(f32[1024,512]{1,0:T(8,128)} %x_ref.1), custom_call_target="tpu_custom_call" | custom-call | tf_op jit(solution)/shard_map/sign/pallas_call | solution.py:494
  307.3 3.1 copy.3

commit v3 on v2

--- a/solution.py
+++ b/solution.py
@@ -29,6 +29,7 @@
         self.total = self.pieces + self.extra
         self.split = (self.w // self.ys) % 128 == 0
         self.cw = self.w // self.ys if self.split else self.w
+        self.bulk = self.ys == 2 and self.q % 2 == 0
 
     def locate(self):
         self.row, self.col = lax.axis_index("row"), lax.axis_index("col")
@@ -103,28 +104,35 @@
             start, offset = piece * plan.ph, plan.offset(plan.row, plan.col, piece)
         return self.x_ref.at[pl.ds(pl.multiple_of(start, plan.ph), plan.ph), pl.ds(offset, plan.pw)]
 
+    def held(self, sy, sc, piece):
+        return self.stage.at[(sy * self.plan.col_n + sc) * self.plan.total + piece]
+
+    def crossed(self, sy, sc, piece):
+        return self.cross.at[(sy * self.plan.col_n + sc) * self.plan.pieces + piece]
+
     def link(self, act, way, src, sy, sc, piece):
-        dst, at = self.stage.at[sy, sc, piece], sy * self.plan.col_n + sc
+        dst, at = self.held(sy, sc, piece), sy * self.plan.col_n + sc
         getattr(pltpu.make_async_remote_copy(
-            src_ref=dst if src is None else src, dst_ref=dst, send_sem=self.send.at[way, at, piece],
+            src_ref=dst if src is None else src, dst_ref=dst,
+            send_sem=self.send.at[way] if self.plan.bulk else self.send.at[way, at, piece],
             recv_sem=self.recv.at[at, piece], device_id=self.ways[way][0], device_id_type=MESH), act)()
 
-    def across(self, act, src, sy, sc, piece):
-        plan, at = self.plan, sy * self.plan.col_n + sc
+    def across(self, src, sy, sc, piece):
+        plan = self.plan
         if not plan.halved:
             return
 
         @pl.when((piece < plan.pieces) & jnp.logical_not(plan.is_mine(sc)))
         def _():
-            getattr(pltpu.make_async_remote_copy(
-                src_ref=self.stage.at[sy, sc, piece] if src is None else src, dst_ref=self.cross.at[sy, sc, piece],
-                send_sem=self.cross_send.at[at, piece], recv_sem=self.cross_recv.at[at, piece],
-                device_id=self.partner, device_id_type=MESH), act)()
+            pltpu.make_async_remote_copy(
+                src_ref=self.held(sy, sc, piece) if src is None else src, dst_ref=self.crossed(sy, sc, piece),
+                send_sem=self.cross_send, recv_sem=self.cross_recv.at[sy * plan.col_n + sc, piece],
+                device_id=self.partner, device_id_type=MESH).start()
 
     def onward(self, act, src, where, piece, spot):
         plan = self.plan
         dx, dy, y_sign, z_sign = where
-        sy, sc, dz, _ = spot
+        sy, sc, dz = spot[:3]
         z_last = piece < plan.pieces // 4
         y_first = lax.rem(piece, 2) == 1
         near = dz == 0
@@ -152,7 +160,7 @@
                 if dy == 0 or y_sign == sign:
                     go(way, y_open)
 
-    def spot(self, where, far, piece):
+    def spot(self, where, far):
         plan = self.plan
         dx, dy, y_sign, z_sign = where
         dz = far - dx - dy
@@ -162,9 +170,13 @@
         there = (dz >= (0 if z_sign > 0 else 1)) & (sz >= 0) & (sz < plan.zs)
         if plan.ys != 2:
             there = there & (sy >= 0) & (sy < plan.ys)
-        if plan.extra:
-            there = there & ((piece < plan.pieces) | plan.is_diagonal(sy, sc))
-        return sy, sc, dz, there
+        return sy, sc, dz, there, plan.is_diagonal(sy, sc) if plan.extra else None
+
+    def has(self, spot, piece):
+        there = spot[3] & (piece >= 0)
+        if self.plan.extra:
+            return there & ((piece < self.plan.pieces) | (spot[4] & (piece < self.plan.total)))
+        return there & (piece < self.plan.total)
 
     def begin(self):
         plan = self.plan
@@ -173,8 +185,8 @@
         def step(extra):
             def start(piece, carry):
                 src = self.own(piece, extra)
-                self.onward("start", src, here, piece, (plan.y, plan.col, jnp.int32(0), None))
-                self.across("start", src, plan.y, plan.col, piece)
+                self.onward("start", src, here, piece, (plan.y, plan.col, jnp.int32(0)))
+                self.across(src, plan.y, plan.col, piece)
                 return carry
             return start
         lax.fori_loop(0, plan.pieces, step(False), 0)
@@ -184,15 +196,15 @@
                 lax.fori_loop(plan.pieces, plan.total, step(True), 0)
 
     def wait_arrival(self, sy, sc, piece):
-        dst = self.stage.at[sy, sc, piece]
+        dst = self.held(sy, sc, piece)
         pltpu.make_async_remote_copy(
-            src_ref=dst, dst_ref=dst, send_sem=self.send.at[0, 0, 0], recv_sem=self.recv.at[sy * self.plan.col_n + sc, piece],
+            src_ref=dst, dst_ref=dst, send_sem=self.send.at[0] if self.plan.bulk else self.send.at[0, 0, 0], recv_sem=self.recv.at[sy * self.plan.col_n + sc, piece],
             device_id=self.ways[0][0], device_id_type=MESH).wait_recv()
 
     def wait_cross(self, sy, sc, piece):
-        dst = self.cross.at[sy, sc, piece]
+        dst = self.crossed(sy, sc, piece)
         pltpu.make_async_remote_copy(
-            src_ref=dst, dst_ref=dst, send_sem=self.cross_send.at[0, 0],
+            src_ref=dst, dst_ref=dst, send_sem=self.cross_send,
             recv_sem=self.cross_recv.at[sy * self.plan.col_n + sc, piece],
             device_id=self.partner, device_id_type=MESH).wait_recv()
 
@@ -228,76 +240,114 @@
 
         def fetch_turned(act, sy, sc, piece, slot, e):
             getattr(pltpu.make_async_copy(
-                self.cross.at[sy, sc, piece], self.turned.at[slot, e], self.turned_sem.at[slot, e]), act)()
-
-        def turn(where, far, piece):
-            sy, sc, dz, there = self.spot(where, far, piece)
-            return sy, sc, there & (piece < plan.pieces) & plan.is_mine(sc)
-
-        def one(far, piece, e, where):
-            slot = lax.rem(far * plan.total + piece, 2)
-            spot = self.spot(where, far, piece)
-            sy, sc, _, there = spot
-
-            @pl.when(there & (far > 0))
+                self.crossed(sy, sc, piece), self.turned.at[slot, e], self.turned_sem.at[slot, e]), act)()
+
+        def arriving(far, piece, slot, e, where, spot):
+            sy, sc = spot[:2]
+
+            @pl.when(self.has(spot, piece) & (far > 0))
             def _():
                 self.wait_arrival(sy, sc, piece)
                 self.onward("start", None, where, piece, spot)
-                self.across("start", None, sy, sc, piece)
-
-            wrap = (piece == 0).astype(jnp.int32)
-            old_far, old_piece = far - wrap, piece - 1 + wrap * plan.total
-            oy, oc, _, old = self.spot(where, old_far, old_piece)
-
-            @pl.when(old)
-            def _():
-                fetch("wait", self.stage.at[oy, oc, old_piece], 1 - slot, e)
-                self.lay(self.tiles.at[1 - slot, e], oy, oc, old_piece)
-
-            @pl.when(there & (far > 0))
-            def _():
-                fetch("start", self.stage.at[sy, sc, piece], slot, e)
+                self.across(None, sy, sc, piece)
+
+            @pl.when(self.has(spot, piece - 1))
+            def _():
+                fetch("wait", self.held(sy, sc, piece - 1), 1 - slot, e)
+                self.lay(self.tiles.at[1 - slot, e], sy, sc, piece - 1)
+
+            @pl.when(self.has(spot, piece) & (far > 0))
+            def _():
+                fetch("start", self.held(sy, sc, piece), slot, e)
             if where == (0, 0, 0, 1):
-                @pl.when(there & (far == 0) & (piece < plan.pieces))
+                @pl.when(self.has(spot, piece) & (far == 0) & (piece < plan.pieces))
                 def _():
                     fetch("start", self.own(piece), slot, e)
                 if plan.extra:
-                    @pl.when(there & (far == 0) & (piece >= plan.pieces))
+                    @pl.when(self.has(spot, piece) & (far == 0) & (piece >= plan.pieces))
                     def _():
                         fetch("start", self.own(piece, True), slot, e)
 
-            if plan.halved:
-                ty, tc, old_turn = turn(where, old_far - 1, old_piece)
-
-                @pl.when(old_turn)
-                def _():
-                    fetch_turned("wait", ty, tc, old_piece, 1 - slot, e)
-                    self.lay_turned(self.turned.at[1 - slot, e], ty, tc, old_piece)
-                uy, uc, new_turn = turn(where, far - 1, piece)
-
-                @pl.when(new_turn)
-                def _():
-                    self.wait_cross(uy, uc, piece)
-                    fetch_turned("start", uy, uc, piece, slot, e)
-                vy, vc, _, sent = self.spot(where, far - 1, piece)
-
-                @pl.when(sent)
-                def _():
-                    self.across("wait_send", None, vy, vc, piece)
-            done = self.spot(where, far - 2, piece)
-
-            @pl.when(done[3])
-            def _():
-                self.onward("wait_send", None, where, piece, done)
+        def crossing(piece, slot, e, spot):
+            sy, sc = spot[:2]
+
+            @pl.when((piece > 0) & (piece <= plan.pieces))
+            def _():
+                fetch_turned("wait", sy, sc, piece - 1, 1 - slot, e)
+                self.lay_turned(self.turned.at[1 - slot, e], sy, sc, piece - 1)
+
+            @pl.when(piece < plan.pieces)
+            def _():
+                self.wait_cross(sy, sc, piece)
+                fetch_turned("start", sy, sc, piece, slot, e)
 
         def round_(far, carry):
+            now = [self.spot(where, far) for where in wheres]
+            before = [self.spot(where, far - 1) for where in wheres]
+
             def step(piece, carry):
+                slot = lax.rem(piece, 2)
                 for e, where in enumerate(wheres):
-                    one(far, piece, e, where)
+                    @pl.when(now[e][3])
+                    def _():
+                        arriving(far, piece, slot, e, where, now[e])
+                    if plan.halved:
+                        @pl.when(before[e][3] & plan.is_mine(before[e][1]))
+                        def _():
+                            crossing(piece, slot, e, before[e])
                 return carry
-            return lax.fori_loop(0, plan.total, step, carry)
+            return lax.fori_loop(0, plan.total + 1, step, carry)
 
         lax.fori_loop(0, plan.zs + plan.ys + 1, round_, 0)
+
+    def finish(self):
+        plan = self.plan
+        if plan.halved:
+            some = self.cross.at[pl.ds(0, plan.ys * plan.col_n // 2 * plan.pieces)]
+            pltpu.make_async_remote_copy(
+                src_ref=some, dst_ref=some, send_sem=self.cross_send, recv_sem=self.cross_recv.at[0, 0],
+                device_id=self.partner, device_id_type=MESH).wait_send()
+        if not plan.bulk:
+            def step(far, carry):
+                def one(piece, carry):
+                    for where in places(plan):
+                        spot = self.spot(where, far)
+
+                        @pl.when(self.has(spot, piece))
+                        def _():
+                            self.onward("wait_send", None, where, piece, spot)
+                    return carry
+                return lax.fori_loop(0, plan.total, one, carry)
+            lax.fori_loop(0, plan.zs + plan.ys, step, 0)
+            return
+
+        def settle(way, count):
+            some = self.stage.at[pl.ds(0, count)]
+            pltpu.make_async_remote_copy(
+                src_ref=some, dst_ref=some, send_sem=self.send.at[way], recv_sem=self.recv.at[0, 0],
+                device_id=self.ways[way][0], device_id_type=MESH).wait_send()
+
+        zs, last, m = plan.zs, plan.pieces // 4, plan.q // 2
+        even_last, odd_last = (last + 1) // 2, last // 2
+        even = (plan.pieces + 1) // 2 - even_last
+        odd = plan.pieces // 2 - odd_last
+        more = range(plan.pieces, plan.total)
+        even_more = sum(p % 2 == 0 for p in more)
+        odd_more = plan.extra - even_more
+        settle(0, zs * (even + 2 * odd) + even_last + 2 * odd_last + m * (even_more + 2 * odd_more))
+        settle(1, zs * (2 * even + odd) + 2 * even_last + odd_last + m * (2 * even_more + odd_more))
+        each = even + odd + 4 * last
+        for way, sign in ((2, 1), (3, -1)):
+            marked = sum(
+                ((sign * (sz - plan.z) >= 0) & (sz // m == 2 * plan.y + plan.core)).astype(jnp.int32) for sz in range(zs))
+            for at in range(zs):
+                spots = zs - at if sign > 0 else at + 1
+                if at == (0 if sign > 0 else zs - 1):
+                    continue
+                for extras in range(m + 1 if plan.extra else 1):
+                    @pl.when((plan.z == at) & (marked == extras if plan.extra else True))
+                    def _():
+                        settle(way, spots * each + extras * plan.extra)
 
 
 STEPS = 8
@@ -475,6 +525,7 @@
             for part in range(CHUNKS):
                 deliver(lax.rem(y + 1 + far_off, plan.ys), far_off, part).wait()
     local.wait()
+    gather.finish()
 
 
 CHUNKS = 2
@@ -484,11 +535,11 @@
     plan = Plan(row_n, col_n, matrix.shape)
     h, half, cw = plan.h, plan.n // 2, plan.cw
     vmem = pltpu.VMEM
-    full, count = (plan.ys, plan.col_n), plan.ys * plan.col_n
+    count, ways = plan.ys * plan.col_n, 4 if plan.ys == 2 else 5
     shapes = [jax.ShapeDtypeStruct((h, plan.w), F32),
-              jax.ShapeDtypeStruct((*full, plan.total, plan.ph, plan.pw), F32)]
+              jax.ShapeDtypeStruct((count * plan.total, plan.ph, plan.pw), F32)]
     if plan.halved:
-        shapes.append(jax.ShapeDtypeStruct((*full, plan.pieces, plan.ph, plan.pw), F32))
+        shapes.append(jax.ShapeDtypeStruct((count * plan.pieces, plan.ph, plan.pw), F32))
     spots = len(places(plan))
     turned = (2, spots, plan.ph, plan.pw) if plan.halved else (8, 128)
     return pl.pallas_call(
@@ -497,8 +548,8 @@
         scratch_shapes=[vmem((half, plan.n), BF16)] * 2 + [vmem((half, cw), BF16)] * 4
         + [vmem((2, half, cw), F32)] * 2 + [vmem((half, cw), F32)] * 2
         + [vmem((2, spots, plan.ph, plan.pw), F32), vmem(turned, F32)] + [vmem((8, 128), F32)] * 3
-        + [DMA((count, plan.total)), DMA((4 if plan.ys == 2 else 5, count, plan.total)), DMA((count, plan.pieces)),
-           DMA((count, plan.pieces)), DMA((2, spots)), DMA((2, spots))]
+        + [DMA((count, plan.total)), DMA((ways,) if plan.bulk else (ways, count, plan.total)),
+           DMA((count, plan.pieces)), DMA(()), DMA((2, spots)), DMA((2, spots))]
         + [DMA((2, plan.ys)), DMA((2, plan.ys)), DMA((2,)), DMA(()), DMA((plan.ys - 1, CHUNKS)),
            DMA((plan.ys - 1, CHUNKS))],
         compiler_params=pltpu.CompilerParams(collective_id=0, has_side_effects=True, vmem_limit_bytes=63 * 2**20),

time: 311 us -> 296 us (0.952)
  Pallas kernels: 307 us -> 292 us
    pallas_call x1, Pallas kernels: 307 us -> 292 us  [shards(): pl.pallas_call(functools.partial(sign_kernel, plan), out_shape=shapes, in...]
where the time goes in v3:
time: 296 us; the launch traced here: 295 us
  Pallas kernels  292 us (99%)
  local copies, waits for them, and re-layouts  3.08 us (1%)
    pallas_call x1, Pallas kernels, shards(): pl.pallas_call(functools.partial(sign_kernel, plan), out_shape=shapes, in...  292 us

profile of v3, /device:TPU:0, one launch (start us, length us, event | category | flops | bytes accessed | tf_op | source)
XLA Modules:
  0.0 295.2 jit_solution(10954859075489057627)
XLA Ops:
  0.0 292.1 %sign.1 = (f32[1024,512]{1,0:T(8,128)}, f32[160,128,256]{2,1,0:T(8,128)}, f32[128,128,256]{2,1,0:T(8,128)}) custom-call(f32[1024,512]{1,0:T(8,128)} %x_ref.1), custom_call_target="tpu_custom_call" | custom-call | tf_op jit(solution)/shard_map/sign/pallas_call | solution.py:545
  292.1 3.1 %copy.3 = f32[1024,512]{1,0:T(8,128)} copy(f32[1024,512]{1,0:T(8,128)} %get-tuple-element.6) | data formatting | bytes 4194304

commit v4 on v3

--- a/solution.py
+++ b/solution.py
@@ -23,7 +23,7 @@
         self.q = self.h // self.w
         self.halved = self.w % 256 == 0
         self.pw = self.w // 2 if self.halved else self.w
-        self.pieces = max(2, self.h * self.pw // 32768)
+        self.pieces = max(2, self.h * self.pw // 65536)
         self.ph = self.h // self.pieces
         self.extra = self.pw // self.ph if self.halved else 0
         self.total = self.pieces + self.extra

time: 296 us -> 281 us (0.949)
  Pallas kernels: 292 us -> 277 us
    pallas_call x1, Pallas kernels: 292 us -> 277 us  [shards(): pl.pallas_call(functools.partial(sign_kernel, plan), out_shape=shapes, in...]
where the time goes in v4:
time: 281 us
  Pallas kernels  277 us (99%)
  local copies, waits for them, and re-layouts  3.08 us (1%)
    pallas_call x1, Pallas kernels, shards(): pl.pallas_call(functools.partial(sign_kernel, plan), out_shape=shapes, in...  277 us

profile of v4, /device:TPU:0, one launch (start us, length us, event | category | flops | bytes accessed | tf_op | source)
XLA Modules:
  0.0 280.6 jit_solution(3491369168411000896)
XLA Ops:
  0.0 277.5 %sign.1 = (f32[1024,512]{1,0:T(8,128)}, f32[80,256,256]{2,1,0:T(8,128)}, f32[64,256,256]{2,1,0:T(8,128)}) custom-call(f32[1024,512]{1,0:T(8,128)} %x_ref.1), custom_call_target="tpu_custom_call" | custom-call | tf_op jit(solution)/shard_map/sign/pallas_call | solution.py:545
  277.5 3.1 %copy.3 = f32[1024,512]{1,0:T(8,128)} copy(f32[1024,512]{1,0:T(8,128)} %get-tuple-element.6) | data formatting | bytes 4194304
